TPU v7x, 128 devices: a whole 4x4x4 slice. The times are simulated.
128 devices in a mesh: batch: 4 (over y), expert: 8 (over x, core), tensor: 4 (over z).
Axes of the slice: x: 4, y: 4, z: 4, core: 2. Of those that a mesh axis runs over, the one named last changes fastest.
Arguments:
- tokens: bfloat16 [8, 1024, 4096], P('expert', 'batch', 'tensor'), may hold values from -8 to 8
- gain: bfloat16 [4096], P('tensor'), may hold values from 0.5 to 1.5
- phi: bfloat16 [4096, 512], P('tensor'), may hold values from -1 to 1
- w_gate: bfloat16 [8, 4096, 14336], P('expert', None, ('batch', 'tensor')), may hold values from -0.125 to 0.125
- w_up: bfloat16 [8, 4096, 14336], P('expert', None, ('batch', 'tensor')), may hold values from -0.125 to 0.125
- w_down: bfloat16 [8, 14336, 4096], P('expert', ('batch', 'tensor')), may hold values from -0.09375 to 0.09375
Outputs:
- moe_out: bfloat16 [8, 1024, 4096], P('expert', 'batch', 'tensor')
All inputs are finite; a program needn't handle non-finite values.
Results may differ from a plain program's by a relative error of at most 0.025.
Values may be sent and summed in bfloat16 or wider, within the bound.
A program may use at most 128 MiB of HBM per device.

v0:
```python
import jax
import jax.numpy as jnp
from jax import lax
from jax.sharding import PartitionSpec as P

D = 4096
P_SIZE = 64


def sent_to_all(x, axis):
    size = lax.axis_size(axis)
    return lax.all_to_all(jnp.broadcast_to(x[None], (size, *x.shape)), axis, 0, 0, tiled=True)


def of_everyone(x, axis):
    return sent_to_all(x, axis).sum(axis=0)


def packed_total(arrays, axis):
    ends = [0]
    for a in arrays:
        ends.append(ends[-1] + a.size)
    running = of_everyone(jnp.concatenate([a.ravel() for a in arrays]), axis)
    return tuple((running[b:e].reshape(a.shape) for a, b, e in zip(arrays, ends, ends[1:])))


def collected_together(x, axis):
    leaves = jax.tree.leaves(x)
    order = sorted(range(len(leaves)), key=lambda k: -leaves[k].size)
    width = (1, *leaves[order[0]].shape)[-1]
    lines = [
        jnp.pad(leaves[k].reshape(-1), (0, -leaves[k].size % width)).reshape(-1, width)
        for k in order
    ]
    both, at, found = (sent_to_all(jnp.concatenate(lines), axis), 0, {})
    for k, line in zip(order, lines):
        piece = both[:, at : at + len(line)].reshape(len(both), -1)
        found[k] = piece[:, : leaves[k].size].reshape(-1, *leaves[k].shape)
        at += len(line)
    numbers = iter(range(len(leaves)))
    return jax.tree.map(lambda _: found[next(numbers)], x)


def combined_pairwise(pieces, combine):
    while len(jax.tree.leaves(pieces)[0]) > 1:
        pieces = jax.vmap(combine)(
            *(jax.tree.map(lambda part: part[side::2], pieces) for side in (0, 1))
        )
    return jax.tree.map(lambda part: part[0], pieces)


def joined_all(x, axis, combine):
    pieces = collected_together(x, axis)
    return combined_pairwise(pieces, combine)


def cut_along(x, dim, size):
    dims = x.shape
    parts = x.reshape(*dims[:dim], size, dims[dim] // size, *dims[dim + 1 :])
    return jnp.moveaxis(parts, dim, 0)


def summed_on_arrival(x, axis, dim):
    size = lax.axis_size(axis)
    parts = lax.all_to_all(cut_along(x, dim, size), axis, 0, 0, tiled=True)
    return jnp.sum(parts.astype(jnp.float32), axis=0)


def laid_out(parts, dim):
    dims = list(parts.shape[1:])
    dims[dim] *= parts.shape[0]
    return jnp.moveaxis(parts, 0, dim).reshape(dims)


def collect(x, axis, dim):
    parts = sent_to_all(x, axis)
    return laid_out(parts, dim)


def joint_totals(left_pair, right_pair):
    new_max = jnp.maximum(left_pair[0], right_pair[0])
    merged = left_pair[1] * jnp.exp(left_pair[0] - new_max) + right_pair[1] * jnp.exp(
        right_pair[0] - new_max
    )
    return (new_max, merged)


def local(tokens, gain, phi, w_gate, w_up, w_down):
    tokens_f = tokens[0].astype(jnp.float32)
    gain_f = gain.astype(jnp.float32)
    scaled = (tokens_f * gain_f[None, :]).astype(jnp.bfloat16)
    squares = jnp.sum(tokens_f * tokens_f, axis=1)
    partial_logits = jnp.dot(scaled, phi, preferred_element_type=jnp.float32)
    squares, partial_logits = packed_total((squares, partial_logits), "tensor")
    inv_rms = lax.rsqrt(squares / D + 1e-06)
    logits = partial_logits * inv_rms[:, None]
    normed = (tokens_f * gain_f[None, :] * inv_rms[:, None]).astype(jnp.bfloat16)
    combine = jax.nn.softmax(logits, axis=1).astype(jnp.bfloat16)
    local_max = jnp.max(logits, axis=0)
    local_total = jnp.sum(jnp.exp(logits - local_max[None, :]), axis=0)
    column_max, column_total = joined_all((local_max, local_total), "batch", joint_totals)
    dispatch = (jnp.exp(logits - column_max[None, :]) / column_total[None, :]).astype(jnp.bfloat16)
    slot_partial = jnp.einsum("ts,td->sd", dispatch, normed, preferred_element_type=jnp.float32)
    per_device = w_gate.shape[0]
    experts = phi.shape[1] // P_SIZE
    width_share = tokens.shape[2]
    slot_partial = slot_partial.reshape(experts, P_SIZE, width_share)
    quarter = summed_on_arrival(slot_partial.astype(jnp.bfloat16), "batch", 1).astype(jnp.bfloat16)
    exchanged = lax.all_to_all(quarter, "expert", split_axis=0, concat_axis=0, tiled=True)
    arrived = collect(exchanged, "batch", 1)
    groups = arrived.shape[0] // per_device
    arrived = arrived.reshape(groups, per_device, P_SIZE, width_share)
    hidden_share = w_gate.shape[2]
    shard_piece = lax.all_gather(arrived, "tensor", axis=3, tiled=True)
    gate_next = jnp.einsum(
        "gxpd,xdf->gxpf", shard_piece, w_gate, preferred_element_type=jnp.float32
    )
    up_next = jnp.einsum("gxpd,xdf->gxpf", shard_piece, w_up, preferred_element_type=jnp.float32)
    hidden = (jax.nn.silu(gate_next) * up_next).astype(jnp.bfloat16)
    batch_count = lax.axis_size("batch")
    tensor_count = lax.axis_size("tensor")
    hidden = hidden.reshape(groups, per_device, batch_count, P_SIZE // batch_count, hidden_share)
    down_split = w_down.reshape(per_device, hidden_share, tensor_count, D // tensor_count)
    partials = jnp.einsum(
        "gxbqf,xftd->btgxqd", hidden, down_split, preferred_element_type=jnp.float32
    )
    partials = partials.reshape(
        batch_count * tensor_count, groups, per_device, P_SIZE // batch_count, width_share
    ).astype(jnp.bfloat16)
    summed = summed_on_arrival(partials, ("batch", "tensor"), 0)
    slot_out = summed[0].astype(jnp.bfloat16)
    returned = lax.all_to_all(slot_out, "expert", split_axis=0, concat_axis=0, tiled=True)
    returned = returned.reshape(experts, P_SIZE // batch_count, width_share)
    returned = collect(returned, "batch", 1)
    moe_out = jnp.dot(
        combine, returned.reshape(experts * P_SIZE, width_share), preferred_element_type=jnp.float32
    )
    return moe_out.astype(jnp.bfloat16)[None]


def solution(mesh):
    placed = (
        P("expert", "batch", "tensor"),
        P("tensor"),
        P("tensor", None),
        P("expert", None, ("batch", "tensor")),
        P("expert", None, ("batch", "tensor")),
        P("expert", ("batch", "tensor"), None),
    )
    return jax.shard_map(
        local, mesh=mesh, in_specs=placed, out_specs=P("expert", "batch", "tensor"), check_vma=False
    )
```

profile of v0, /device:TPU:0, one launch (start us, length us, event | category | flops | bytes accessed | tf_op | source)
XLA Modules:
  0.0 282.4 jit_solution(13784396119925911884)
XLA Ops:
  6.5 1.3 fusion.22
  8.5 1.5 convolution_bitcast_fusion
  10.2 2.5 broadcast_in_dim.12
  12.8 31.6 %all_to_all.41 = f32[4,1,131328]{2,1,0:T(1,128)S(1)} all-to-all(f32[4,1,131328]{2,1,0:T(1,128)S(1)} %broadcast_in_dim.12), channel_id=1, replica_groups=mesh['batch'=4,'expert'=8,'tensor'=4] {'tensor'}, dimensions={0} | all-to-all | bytes 4202496 | tf_op jit(solution)/shard_map/all_to_all | solution.py:12
  44.4 10.6 %reduce_sum.61 = f32[131328]{0:T(1024)} reduce(f32[4,1,131328]{2,1,0:T(1,128)S(1)} %all_to_all.41, f32[]{:T(128)} %constant.6.clone.1), dimensions={0,1}, to_apply=%region_1.0 | reduce | flops 393984 | bytes 2626564 | tf_op jit(solution)/shard_map/reduce_sum | solution.py:16
  55.7 1.1 slice.52
  57.4 9.6 %all_to_all.42 = f32[4,2,512]{2,1,0:T(2,128)S(1)} all-to-all(f32[4,2,512]{2,1,0:T(2,128)S(1)} %broadcast_in_dim.13), channel_id=1, replica_groups=mesh['batch'=4,'expert'=8,'tensor'=4] {'batch'}, dimensions={0} | all-to-all | bytes 32768 | tf_op jit(solution)/shard_map/all_to_all | solution.py:12
  68.1 15.2 %all_to_all.43 = bf16[4,8,16,1024]{3,2,1,0:T(8,128)(2,1)S(1)} all-to-all(bf16[4,8,16,1024]{3,2,1,0:T(8,128)(2,1)S(1)} %bitcast.118), channel_id=1, replica_groups=mesh['batch'=4,'expert'=8,'tensor'=4] {'batch'}, dimensions={0} | all-to-all | bytes 2097152 | tf_op jit(solution)/shard_map/all_to_all | solution.py:65
  83.5 11.6 %all_to_all.44 = bf16[8,16,1024]{2,1,0:T(8,128)(2,1)S(1)} all-to-all(bf16[8,16,1024]{2,1,0:T(8,128)(2,1)S(1)} %reduce_sum.64), channel_id=1, replica_groups=mesh['batch'=4,'expert'=8,'tensor'=4] {'expert'}, dimensions={0} | all-to-all | bytes 524288 | tf_op jit(solution)/shard_map/all_to_all | solution.py:109
  95.2 17.4 %all_to_all.45 = bf16[4,8,16,1024]{3,2,1,0:T(8,128)(2,1)S(1)} all-to-all(bf16[4,8,16,1024]{3,2,1,0:T(8,128)(2,1)S(1)} %broadcast_in_dim.14), channel_id=1, replica_groups=mesh['batch'=4,'expert'=8,'tensor'=4] {'batch'}, dimensions={0} | all-to-all | bytes 2097152 | tf_op jit(solution)/shard_map/all_to_all | solution.py:12
  113.7 13.1 %reshape.131 = bf16[896,4,1024]{2,1,0:T(4,128)(2,1)} reshape(bf16[1,896,4096]{2,1,0:T(8,128)(2,1)} %param.11) | data formatting | bytes 14680064 | tf_op jit(solution)/shard_map/reshape.6
  126.8 31.1 %all-gather.2.cloned.1.call-done = bf16[8,1,64,4096]{3,2,0,1:T(8,128)(2,1)} async-done(((bf16[8,1,64,1024]{3,2,0,1:T(8,128)(2,1)}), bf16[8,1,64,4096]{3,2,0,1:T(8,128)(2,1)}) %all-gather.2.cloned.1.call-update) | async-done | bytes 4194320 | tf_op jit(solution)/shard_map/all_gather | solution.py:114
  157.9 10.5 %fusion.4 = f32[8,64,896]{2,1,0:T(8,128)S(1)} fusion(bf16[1,4096,896]{2,1,0:T(8,128)(2,1)} %param.9, bf16[8,1,64,4096]{3,2,0,1:T(8,128)(2,1)} %all-gather.2.cloned.1.call-done), kind=kOutput, calls=%fused_computation.4 | convolution fusion | flops 3758096384 | bytes 13369344 | tf_op jit(solution)/shard_map/gxpd,xdf->gxpf/dot_general | solution.py:115
  168.5 7.8 %fusion.11 = bf16[8,1,64,896]{3,2,0,1:T(8,128)(2,1)S(1)} fusion(f32[8,64,896]{2,1,0:T(8,128)S(1)} %fusion.4, bf16[1,4096,896]{2,1,0:T(8,128)(2,1)} %param.10, bf16[8,1,64,4096]{3,2,0,1:T(8,128)(2,1)S(1)} %copy-done.4), kind=kOutput, calls=%fused_computation.10 | convolution fusion | flops 3760848896 | bytes 14286848 | tf_op jit(solution)/shard_map/gxpd,xdf->gxpf/dot_general | solution.py:118
  176.3 5.6 %fusion.8 = bf16[8,4,16,4,1024]{4,2,3,1,0:T(8,128)(2,1)S(1)} fusion(bf16[8,4,16,896,1]{3,2,4,1,0:T(8,128)(2,1)S(1)} %bitcast.130, bf16[896,4,1024,1,1]{2,1,0,4,3:T(4,128)(2,1)S(1)} %bitcast.113), kind=kOutput, calls=%fused_computation.8 | convolution fusion | flops 3760193536 | bytes 12451840 | tf_op jit(solution)/shard_map/gxbqf,xftd->btgxqd/dot_general | solution.py:124
  182.4 56.5 %all_to_all.46 = bf16[16,1,8,1,16,1024]{5,4,2,3,1,0:T(8,128)(2,1)} all-to-all(bf16[16,1,8,1,16,1024]{5,4,2,3,1,0:T(8,128)(2,1)S(1)} %copy.35), channel_id=1, replica_groups=mesh['batch'=4,'expert'=8,'tensor'=4] {'batch','tensor'}, dimensions={0} | all-to-all | bytes 8388608 | tf_op jit(solution)/shard_map/all_to_all | solution.py:65
  238.8 3.9 %reduce_sum.65 = bf16[8,16,1024]{2,1,0:T(8,128)(2,1)} reduce(bf16[16,1,8,1,16,1024]{5,4,2,3,1,0:T(8,128)(2,1)} %all_to_all.46, bf16[]{:T(256)} %constant.15.clone.1), dimensions={0,1,3}, to_apply=%region_7.8 | reduce | flops 1966080 | bytes 4456450 | tf_op jit(solution)/shard_map/reduce_sum | solution.py:66
  242.7 4.4 %all-to-all-start.6 = ((bf16[8,1,16,1024]{3,2,1,0:T(8,128)(2,1)}), bf16[8,1,16,1024]{3,2,1,0:T(8,128)(2,1)S(1)}, u32[]{:S(2)}, u32[]{:S(2)}) async-start(bf16[8,1,16,1024]{3,2,1,0:T(8,128)(2,1)} %bitcast.35), calls=%async_computation.6 | async-start | bytes 524288 | tf_op jit(solution)/shard_map/all_to_all | solution.py:132
  250.0 4.6 %all-to-all-done.6 = bf16[8,1,16,1024]{3,2,1,0:T(8,128)(2,1)S(1)} async-done(((bf16[8,1,16,1024]{3,2,1,0:T(8,128)(2,1)}), bf16[8,1,16,1024]{3,2,1,0:T(8,128)(2,1)S(1)}, u32[]{:S(2)}, u32[]{:S(2)}) %all-to-all-start.6) | async-done | bytes 262176 | tf_op jit(solution)/shard_map/all_to_all | solution.py:132
  254.6 1.1 broadcast_in_dim.16
  255.7 3.5 %all-to-all-start.7 = ((bf16[4,8,16,1024]{3,2,1,0:T(8,128)(2,1)}), bf16[4,8,16,1024]{3,2,1,0:T(8,128)(2,1)S(1)}, u32[]{:S(2)}, u32[]{:S(2)}) async-start(bf16[4,8,16,1024]{3,2,1,0:T(8,128)(2,1)} %broadcast_in_dim.16), calls=%async_computation.7 | async-start | bytes 2097152 | tf_op jit(solution)/shard_map/all_to_all | solution.py:12
  259.3 1.5 divide_convert_fusion.1
  260.9 13.3 %all-to-all-done.7 = bf16[4,8,16,1024]{3,2,1,0:T(8,128)(2,1)S(1)} async-done(((bf16[4,8,16,1024]{3,2,1,0:T(8,128)(2,1)}), bf16[4,8,16,1024]{3,2,1,0:T(8,128)(2,1)S(1)}, u32[]{:S(2)}, u32[]{:S(2)}) %all-to-all-start.7) | async-done | bytes 1048608 | tf_op jit(solution)/shard_map/all_to_all | solution.py:12
  274.3 1.2 fusion.21
  (48 shorter events, 8.2 us)
Async XLA Ops:
  6.5 2.0 copy-start
  6.5 151.4 %all-gather.2.cloned.1.call-start = ((), (), s32[]{:S(2)}) async-start(), calls=%async_computation.8 | async-start | bytes 5242880 | tf_op jit(solution)/shard_map/all_gather | solution.py:114
  44.4 23.1 %copy-start.2 = (bf16[1,256,1024]{2,1,0:T(8,128)(2,1)S(1)}, bf16[1,256,1024]{2,1,0:T(8,128)(2,1)}, u32[]{:S(2)}) copy-start(bf16[1,256,1024]{2,1,0:T(8,128)(2,1)} %param.6) | copy-start | bytes 1572868
  157.9 10.5 %copy-start.4 = (bf16[8,1,64,4096]{3,2,0,1:T(8,128)(2,1)S(1)}, bf16[8,1,64,4096]{3,2,0,1:T(8,128)(2,1)}, u32[]{:S(2)}) copy-start(bf16[8,1,64,4096]{3,2,0,1:T(8,128)(2,1)} %all-gather.2.cloned.1.call-done) | copy-start | bytes 12582916
  157.9 18.3 %slice-start = ((s8[7340032]{0:T(1024)(128)(4,1)}), s8[4194304]{0:T(1024)(128)(4,1)S(1)}, s32[]{:S(2)}) async-start(s8[7340032]{0:T(1024)(128)(4,1)} %bitcast.111), calls=%async_computation.9 | async-start | bytes 8388608
  168.5 7.8 %slice-start.1 = ((s8[7340032]{0:T(1024)(128)(4,1)}), s8[3145728]{0:T(1024)(128)(4,1)S(1)}, s32[]{:S(2)}) async-start(s8[7340032]{0:T(1024)(128)(4,1)} %bitcast.111), calls=%async_computation.10 | async-start | bytes 6291456
  242.7 16.5 %copy-start.3 = (f32[131328]{0:T(1024)S(1)}, f32[131328]{0:T(1024)}, u32[]{:S(2)}) copy-start(f32[131328]{0:T(1024)} %reduce_sum.61) | copy-start | bytes 1575940
  242.7 11.9 %all-to-all-start.6 = ((bf16[8,1,16,1024]{3,2,1,0:T(8,128)(2,1)}), bf16[8,1,16,1024]{3,2,1,0:T(8,128)(2,1)S(1)}, u32[]{:S(2)}, u32[]{:S(2)}) async-start(bf16[8,1,16,1024]{3,2,1,0:T(8,128)(2,1)} %bitcast.35), calls=%async_computation.6 | async-start | bytes 524288 | tf_op jit(solution)/shard_map/all_to_all | solution.py:132
  254.6 21.0 %copy-start.1 = (bf16[1024,512]{1,0:T(8,128)(2,1)S(1)}, bf16[1024,512]{1,0:T(8,128)(2,1)}, u32[]{:S(2)}) copy-start(bf16[1024,512]{1,0:T(8,128)(2,1)} %param.8) | copy-start | bytes 3145732
  255.7 18.5 %all-to-all-start.7 = ((bf16[4,8,16,1024]{3,2,1,0:T(8,128)(2,1)}), bf16[4,8,16,1024]{3,2,1,0:T(8,128)(2,1)S(1)}, u32[]{:S(2)}, u32[]{:S(2)}) async-start(bf16[4,8,16,1024]{3,2,1,0:T(8,128)(2,1)} %broadcast_in_dim.16), calls=%async_computation.7 | async-start | bytes 2097152 | tf_op jit(solution)/shard_map/all_to_all | solution.py:12
Sparse Core Ops, SparseCore 0:
  113.8 44.0 all-gather.1
where the time goes:
time: 283 us; the launch traced here: 282 us
  blocking collectives  142 us (50%)
  waiting for transfers between devices  49 us (17%)
  matrix products  27.2 us (10%)
  local copies, waits for them, and re-layouts  23.2 us (8%)
  other arithmetic  19.6 us (7%)
  between operations  13.7 us (5%)
  starting transfers between devices  7.9 us (3%)
    all_to_all x2, blocking collectives, summed_on_arrival(): parts = lax.all_to_all(cut_along(x, dim, size), axis, 0, 0, tiled=True)  71.6 us
    all_to_all x3, blocking collectives, sent_to_all(): lax.all_to_all(jnp.broadcast_to(x[None], (size, *x.shape)), axis, 0, 0, t...  58.7 us
    all_gather x1, waiting for transfers between devices, local(): shard_piece = lax.all_gather(arrived, 'tensor', axis=3, tiled=True)  31.1 us
    all_to_all x1, waiting for transfers between devices, sent_to_all(): lax.all_to_all(jnp.broadcast_to(x[None], (size, *x.shape)), axis, 0, 0, t...  13.3 us
    another operation x1, local copies, waits for them, and re-layouts  13.1 us
    all_to_all x1, blocking collectives, local(): lax.all_to_all(quarter, 'expert', split_axis=0, concat_axis=0, tiled=True)  11.6 us
    reduce_sum x1, other arithmetic, of_everyone(): return sent_to_all(x, axis).sum(axis=0)  10.6 us
    dot_general x1, matrix products, local(): jnp.einsum('gxpd,xdf->gxpf', shard_piece, w_gate, preferred_element_type=...  10.5 us
  transfers between devices with their start and end apart: 3, of which 3 were waited for; matrix products, arithmetic and copies ran while one was open for 6% of the time, Pallas kernels for 0%

commit v1 on v0

--- a/solution.py
+++ b/solution.py
@@ -111,7 +111,8 @@
     groups = arrived.shape[0] // per_device
     arrived = arrived.reshape(groups, per_device, P_SIZE, width_share)
     hidden_share = w_gate.shape[2]
-    shard_piece = lax.all_gather(arrived, "tensor", axis=3, tiled=True)
+    copies = jnp.concatenate([arrived] * lax.axis_size("tensor"), axis=3)
+    shard_piece = lax.all_to_all(copies, "tensor", 3, 3, tiled=True)
     gate_next = jnp.einsum(
         "gxpd,xdf->gxpf", shard_piece, w_gate, preferred_element_type=jnp.float32
     )

time: 283 us -> 314 us (1.11)
  local copies, waits for them, and re-layouts: 23.2 us -> 60.6 us
  between operations: 13.7 us -> 0.29 us
  starting transfers between devices: 7.9 us -> 12.2 us
  blocking collectives: 142 us -> 138 us
  waiting for transfers between devices: 49 us -> 52.7 us
    all_to_all x0 -> x1, waiting for transfers between devices: none -> 34.9 us  [local(): shard_piece = lax.all_to_all(copies, 'tensor', 3, 3, tiled=True)]
    all_gather x1 -> x0, waiting for transfers between devices: 31.1 us -> none  [local(): shard_piece = lax.all_gather(arrived, 'tensor', axis=3, tiled=True)]
    unnamed x19 -> x21, local copies, waits for them, and re-layouts: 3.09 us -> 21.9 us
    concatenate x0 -> x1, local copies, waits for them, and re-layouts: none -> 10.1 us  [local(): copies = jnp.concatenate([arrived] * lax.axis_size('tensor'), axis=3)]
    all_to_all x0 -> x1, local copies, waits for them, and re-layouts: none -> 9.77 us  [local(): shard_piece = lax.all_to_all(copies, 'tensor', 3, 3, tiled=True)]
    all_to_all x0 -> x1, starting transfers between devices: none -> 5.12 us  [local(): shard_piece = lax.all_to_all(copies, 'tensor', 3, 3, tiled=True)]
    all_to_all x2, blocking collectives: 71.6 us -> 67.6 us  [summed_on_arrival(): parts = lax.all_to_all(cut_along(x, dim, size), axis, 0, 0, tiled=True)]
where the time goes in v1:
time: 314 us; the launch traced here: 312 us
  blocking collectives  138 us (44%)
  local copies, waits for them, and re-layouts  60.6 us (19%)
  waiting for transfers between devices  52.7 us (17%)
  matrix products  26.6 us (8%)
  other arithmetic  21.8 us (7%)
  starting transfers between devices  12.2 us (4%)
    all_to_all x2, blocking collectives, summed_on_arrival(): parts = lax.all_to_all(cut_along(x, dim, size), axis, 0, 0, tiled=True)  67.6 us
    all_to_all x3, blocking collectives, sent_to_all(): lax.all_to_all(jnp.broadcast_to(x[None], (size, *x.shape)), axis, 0, 0, t...  58.7 us
    all_to_all x1, waiting for transfers between devices, local(): shard_piece = lax.all_to_all(copies, 'tensor', 3, 3, tiled=True)  34.9 us
    unnamed x21, local copies, waits for them, and re-layouts  21.9 us
    all_to_all x1, waiting for transfers between devices, sent_to_all(): lax.all_to_all(jnp.broadcast_to(x[None], (size, *x.shape)), axis, 0, 0, t...  13.3 us
    another operation x1, local copies, waits for them, and re-layouts  12.8 us
    all_to_all x1, blocking collectives, local(): lax.all_to_all(quarter, 'expert', split_axis=0, concat_axis=0, tiled=True)  11.6 us
    reduce_sum x1, other arithmetic, of_everyone(): return sent_to_all(x, axis).sum(axis=0)  10.5 us
  transfers between devices with their start and end apart: 3, of which 3 were waited for; matrix products, arithmetic and copies ran while one was open for 6% of the time, Pallas kernels for 0%

profile of v1, /device:TPU:0, one launch (start us, length us, event | category | flops | bytes accessed | tf_op | source)
XLA Modules:
  0.0 311.9 jit_solution(13801155072609964513)
XLA Ops:
  3.7 2.5 broadcast_in_dim.12
  6.2 31.6 %all_to_all.46 = f32[4,1,131328]{2,1,0:T(1,128)S(1)} all-to-all(f32[4,1,131328]{2,1,0:T(1,128)S(1)} %broadcast_in_dim.12), channel_id=1, replica_groups=mesh['batch'=4,'expert'=8,'tensor'=4] {'tensor'}, dimensions={0} | all-to-all | bytes 4202496 | tf_op jit(solution)/shard_map/all_to_all | solution.py:12
  37.9 10.5 %reduce_sum.61 = f32[131328]{0:T(1024)} reduce(f32[4,1,131328]{2,1,0:T(1,128)S(1)} %all_to_all.46, f32[]{:T(128)} %constant.6.clone.1), dimensions={0,1}, to_apply=%region_1.0 | reduce | flops 393984 | bytes 2626564 | tf_op jit(solution)/shard_map/reduce_sum | solution.py:16
  50.8 9.6 %all_to_all.47 = f32[4,2,512]{2,1,0:T(2,128)S(1)} all-to-all(f32[4,2,512]{2,1,0:T(2,128)S(1)} %broadcast_in_dim.13), channel_id=1, replica_groups=mesh['batch'=4,'expert'=8,'tensor'=4] {'batch'}, dimensions={0} | all-to-all | bytes 32768 | tf_op jit(solution)/shard_map/all_to_all | solution.py:12
  61.5 15.2 %all_to_all.48 = bf16[4,8,16,1024]{3,2,1,0:T(8,128)(2,1)S(1)} all-to-all(bf16[4,8,16,1024]{3,2,1,0:T(8,128)(2,1)S(1)} %bitcast.123), channel_id=1, replica_groups=mesh['batch'=4,'expert'=8,'tensor'=4] {'batch'}, dimensions={0} | all-to-all | bytes 2097152 | tf_op jit(solution)/shard_map/all_to_all | solution.py:65
  76.9 11.6 %all_to_all.49 = bf16[8,16,1024]{2,1,0:T(8,128)(2,1)S(1)} all-to-all(bf16[8,16,1024]{2,1,0:T(8,128)(2,1)S(1)} %reduce_sum.64), channel_id=1, replica_groups=mesh['batch'=4,'expert'=8,'tensor'=4] {'expert'}, dimensions={0} | all-to-all | bytes 524288 | tf_op jit(solution)/shard_map/all_to_all | solution.py:109
  88.6 17.4 %all_to_all.50 = bf16[4,8,16,1024]{3,2,1,0:T(8,128)(2,1)S(1)} all-to-all(bf16[4,8,16,1024]{3,2,1,0:T(8,128)(2,1)S(1)} %broadcast_in_dim.14), channel_id=1, replica_groups=mesh['batch'=4,'expert'=8,'tensor'=4] {'batch'}, dimensions={0} | all-to-all | bytes 2097152 | tf_op jit(solution)/shard_map/all_to_all | solution.py:12
  106.1 2.2 pad_maximum_fusion
  108.3 10.1 %copy.45 = bf16[8,1,64,4096]{2,0,1,3:T(8,128)(2,1)} copy(bf16[8,1,64,4096]{3,2,0,1:T(8,128)(2,1)} %pad_maximum_fusion) | data formatting | bytes 8388608 | tf_op jit(solution)/shard_map/concatenate | solution.py:114
  118.4 9.5 %reshape.138 = bf16[4,2,262144]{2,1,0:T(2,128)(2,1)} reshape(bf16[4096,1,8,64]{3,2,1,0:T(8,128)(2,1)} %bitcast.114) | data formatting | bytes 8388608
  128.0 5.1 %all-to-all-start.5 = ((bf16[4,2,262144]{2,1,0:T(2,128)(2,1)}), bf16[4,2,262144]{2,1,0:T(2,128)(2,1)}, u32[]{:S(2)}, u32[]{:S(2)}) async-start(bf16[4,2,262144]{2,1,0:T(2,128)(2,1)} %reshape.138), calls=%async_computation.5 | async-start | bytes 8388608 | tf_op jit(solution)/shard_map/all_to_all | solution.py:115
  133.1 12.8 %reshape.131 = bf16[896,4,1024]{2,1,0:T(4,128)(2,1)} reshape(bf16[1,896,4096]{2,1,0:T(8,128)(2,1)} %param.11) | data formatting | bytes 14680064 | tf_op jit(solution)/shard_map/reshape.6
  145.9 34.9 %all-to-all-done.5 = bf16[4,2,262144]{2,1,0:T(2,128)(2,1)} async-done(((bf16[4,2,262144]{2,1,0:T(2,128)(2,1)}), bf16[4,2,262144]{2,1,0:T(2,128)(2,1)}, u32[]{:S(2)}, u32[]{:S(2)}) %all-to-all-start.5) | async-done | bytes 4194336 | tf_op jit(solution)/shard_map/all_to_all | solution.py:115
  180.8 9.3 %reshape.139 = bf16[4096,1,8,64]{3,2,1,0:T(8,128)(2,1)} reshape(bf16[4,2,262144]{2,1,0:T(2,128)(2,1)} %all-to-all-done.5) | data formatting | bytes 8388608
  190.1 9.8 %copy.46 = bf16[8,1,64,4096]{3,2,0,1:T(8,128)(2,1)} copy(bf16[8,1,64,4096]{2,0,1,3:T(8,128)(2,1)} %bitcast.115) | data formatting | bytes 8388608 | tf_op jit(solution)/shard_map/all_to_all | solution.py:115
  199.8 9.9 %fusion.4 = f32[8,64,896]{2,1,0:T(8,128)S(1)} fusion(bf16[1,4096,896]{2,1,0:T(8,128)(2,1)} %param.9, bf16[8,1,64,4096]{3,2,0,1:T(8,128)(2,1)} %copy.46), kind=kOutput, calls=%fused_computation.4 | convolution fusion | flops 3758096384 | bytes 13369344 | tf_op jit(solution)/shard_map/gxpd,xdf->gxpf/dot_general | solution.py:116
  209.8 7.8 %fusion.11 = bf16[8,1,64,896]{3,2,0,1:T(8,128)(2,1)S(1)} fusion(f32[8,64,896]{2,1,0:T(8,128)S(1)} %fusion.4, bf16[1,4096,896]{2,1,0:T(8,128)(2,1)} %param.10, bf16[8,1,64,4096]{3,2,0,1:T(8,128)(2,1)S(1)} %copy-done.4), kind=kOutput, calls=%fused_computation.11 | convolution fusion | flops 3760848896 | bytes 14286848 | tf_op jit(solution)/shard_map/gxpd,xdf->gxpf/dot_general | solution.py:119
  217.6 5.7 %fusion.8 = bf16[8,4,16,4,1024]{4,2,3,1,0:T(8,128)(2,1)S(1)} fusion(bf16[8,4,16,896,1]{3,2,4,1,0:T(8,128)(2,1)S(1)} %bitcast.134, bf16[896,4,1024,1,1]{2,1,0,4,3:T(4,128)(2,1)S(1)} %bitcast.118), kind=kOutput, calls=%fused_computation.9 | convolution fusion | flops 3760193536 | bytes 12451840 | tf_op jit(solution)/shard_map/gxbqf,xftd->btgxqd/dot_general | solution.py:125
  223.7 52.4 %all_to_all.51 = bf16[16,1,8,1,16,1024]{5,4,2,3,1,0:T(8,128)(2,1)} all-to-all(bf16[16,1,8,1,16,1024]{5,4,2,3,1,0:T(8,128)(2,1)S(1)} %copy.48), channel_id=1, replica_groups=mesh['batch'=4,'expert'=8,'tensor'=4] {'batch','tensor'}, dimensions={0} | all-to-all | bytes 8388608 | tf_op jit(solution)/shard_map/all_to_all | solution.py:65
  276.1 3.9 %reduce_sum.65 = bf16[8,16,1024]{2,1,0:T(8,128)(2,1)} reduce(bf16[16,1,8,1,16,1024]{5,4,2,3,1,0:T(8,128)(2,1)} %all_to_all.51, bf16[]{:T(256)} %constant.15.clone.1), dimensions={0,1,3}, to_apply=%region_7.8 | reduce | flops 1966080 | bytes 4456450 | tf_op jit(solution)/shard_map/reduce_sum | solution.py:66
  280.0 3.5 %all-to-all-start.7 = ((bf16[8,1,16,1024]{3,2,1,0:T(8,128)(2,1)}), bf16[8,1,16,1024]{3,2,1,0:T(8,128)(2,1)S(1)}, u32[]{:S(2)}, u32[]{:S(2)}) async-start(bf16[8,1,16,1024]{3,2,1,0:T(8,128)(2,1)} %bitcast.35), calls=%async_computation.7 | async-start | bytes 524288 | tf_op jit(solution)/shard_map/all_to_all | solution.py:133
  286.5 4.5 %all-to-all-done.7 = bf16[8,1,16,1024]{3,2,1,0:T(8,128)(2,1)S(1)} async-done(((bf16[8,1,16,1024]{3,2,1,0:T(8,128)(2,1)}), bf16[8,1,16,1024]{3,2,1,0:T(8,128)(2,1)S(1)}, u32[]{:S(2)}, u32[]{:S(2)}) %all-to-all-start.7) | async-done | bytes 262176 | tf_op jit(solution)/shard_map/all_to_all | solution.py:133
  292.1 3.5 %all-to-all-start.8 = ((bf16[4,8,16,1024]{3,2,1,0:T(8,128)(2,1)}), bf16[4,8,16,1024]{3,2,1,0:T(8,128)(2,1)S(1)}, u32[]{:S(2)}, u32[]{:S(2)}) async-start(bf16[4,8,16,1024]{3,2,1,0:T(8,128)(2,1)} %broadcast_in_dim.16), calls=%async_computation.8 | async-start | bytes 2097152 | tf_op jit(solution)/shard_map/all_to_all | solution.py:12
  297.3 13.3 %all-to-all-done.8 = bf16[4,8,16,1024]{3,2,1,0:T(8,128)(2,1)S(1)} async-done(((bf16[4,8,16,1024]{3,2,1,0:T(8,128)(2,1)}), bf16[4,8,16,1024]{3,2,1,0:T(8,128)(2,1)S(1)}, u32[]{:S(2)}, u32[]{:S(2)}) %all-to-all-start.8) | async-done | bytes 1048608 | tf_op jit(solution)/shard_map/all_to_all | solution.py:12
  (52 shorter events, 15.0 us)
Async XLA Ops:
  0.0 2.0 copy-start
  37.8 23.1 %copy-start.2 = (bf16[1,256,1024]{2,1,0:T(8,128)(2,1)S(1)}, bf16[1,256,1024]{2,1,0:T(8,128)(2,1)}, u32[]{:S(2)}) copy-start(bf16[1,256,1024]{2,1,0:T(8,128)(2,1)} %param.6) | copy-start | bytes 1572868
  128.0 52.9 %all-to-all-start.5 = ((bf16[4,2,262144]{2,1,0:T(2,128)(2,1)}), bf16[4,2,262144]{2,1,0:T(2,128)(2,1)}, u32[]{:S(2)}, u32[]{:S(2)}) async-start(bf16[4,2,262144]{2,1,0:T(2,128)(2,1)} %reshape.138), calls=%async_computation.5 | async-start | bytes 8388608 | tf_op jit(solution)/shard_map/all_to_all | solution.py:115
  199.8 9.9 %copy-start.4 = (bf16[8,1,64,4096]{3,2,0,1:T(8,128)(2,1)S(1)}, bf16[8,1,64,4096]{3,2,0,1:T(8,128)(2,1)}, u32[]{:S(2)}) copy-start(bf16[8,1,64,4096]{3,2,0,1:T(8,128)(2,1)} %copy.46) | copy-start | bytes 12582916
  199.8 17.7 %slice-start = ((s8[7340032]{0:T(1024)(128)(4,1)}), s8[4194304]{0:T(1024)(128)(4,1)S(1)}, s32[]{:S(2)}) async-start(s8[7340032]{0:T(1024)(128)(4,1)} %bitcast.116), calls=%async_computation.9 | async-start | bytes 8388608
  209.8 7.8 %slice-start.1 = ((s8[7340032]{0:T(1024)(128)(4,1)}), s8[3145728]{0:T(1024)(128)(4,1)S(1)}, s32[]{:S(2)}) async-start(s8[7340032]{0:T(1024)(128)(4,1)} %bitcast.116), calls=%async_computation.10 | async-start | bytes 6291456
  280.0 15.6 %copy-start.3 = (f32[131328]{0:T(1024)S(1)}, f32[131328]{0:T(1024)}, u32[]{:S(2)}) copy-start(f32[131328]{0:T(1024)} %reduce_sum.61) | copy-start | bytes 1575940
  280.0 11.0 %all-to-all-start.7 = ((bf16[8,1,16,1024]{3,2,1,0:T(8,128)(2,1)}), bf16[8,1,16,1024]{3,2,1,0:T(8,128)(2,1)S(1)}, u32[]{:S(2)}, u32[]{:S(2)}) async-start(bf16[8,1,16,1024]{3,2,1,0:T(8,128)(2,1)} %bitcast.35), calls=%async_computation.7 | async-start | bytes 524288 | tf_op jit(solution)/shard_map/all_to_all | solution.py:133
  291.0 21.0 %copy-start.1 = (bf16[1024,512]{1,0:T(8,128)(2,1)S(1)}, bf16[1024,512]{1,0:T(8,128)(2,1)}, u32[]{:S(2)}) copy-start(bf16[1024,512]{1,0:T(8,128)(2,1)} %param.8) | copy-start | bytes 3145732
  292.1 18.5 %all-to-all-start.8 = ((bf16[4,8,16,1024]{3,2,1,0:T(8,128)(2,1)}), bf16[4,8,16,1024]{3,2,1,0:T(8,128)(2,1)S(1)}, u32[]{:S(2)}, u32[]{:S(2)}) async-start(bf16[4,8,16,1024]{3,2,1,0:T(8,128)(2,1)} %broadcast_in_dim.16), calls=%async_computation.8 | async-start | bytes 2097152 | tf_op jit(solution)/shard_map/all_to_all | solution.py:12
